TPU v7x, 128 devices: a whole 4x4x4 slice. The times are simulated.
128 devices in a mesh: dp: 1, tp: 16 (over z, y), ep: 8 (over x, core).
Axes of the slice: x: 4, y: 4, z: 4, core: 2. Of those that a mesh axis runs over, the one named last changes fastest.
Arguments:
- tokens: bfloat16 [49152, 2048], P(('dp', 'ep', 'tp'))
- expert_ids: int32 [49152, 6], P(('dp', 'ep', 'tp'))
- gates: float32 [49152, 6], P(('dp', 'ep', 'tp'))
- slots: int32 [49152, 6], P(('dp', 'ep', 'tp'))
- shared_w1: bfloat16 [2048, 2816], P(None, 'tp')
- shared_w3: bfloat16 [2048, 2816], P(None, 'tp')
- shared_w2: bfloat16 [2816, 2048], P('tp')
- expert_w1: bfloat16 [64, 2048, 1408], P('ep')
- expert_w3: bfloat16 [64, 2048, 1408], P('ep')
- expert_w2: bfloat16 [64, 1408, 2048], P('ep')
Outputs:
- output: bfloat16 [49152, 2048], P(('dp', 'ep', 'tp'))
All inputs are finite; a program needn't handle non-finite values.
Results may differ from a plain program's by a relative error of at most 0.00146.
Values are sent between devices in bfloat16 or wider.
A program may use at most 1 GiB of HBM per device.

v0:
```python
import jax
import jax.numpy as jnp
from jax import lax
from jax.sharding import PartitionSpec as P


def capacity_rows(tok_dev, top_k, n_exp):
    return 8 * max(1, (2 * tok_dev * top_k + 8 * n_exp - 1) // (8 * n_exp))


def swiglu_rows(token_rows, w_gate, w_up, w_down):
    gate_pre = jnp.dot(token_rows, w_gate, preferred_element_type=jnp.float32)
    up_pre = jnp.dot(token_rows, w_up, preferred_element_type=jnp.float32)
    hidden = (jax.nn.silu(gate_pre) * up_pre).astype(jnp.bfloat16)
    return jnp.dot(hidden, w_down, preferred_element_type=jnp.float32)


def solution(mesh):
    ep_size = mesh.shape["ep"]
    row_spec = P(("dp", "ep", "tp"), None)
    expert_spec = P("ep", None, None)

    def local_layer(tokens, expert_ids, gates, slots, shared_w1, shared_w3, shared_w2, expert_w1, expert_w3, expert_w2):
        tok_dev, d_model = tokens.shape
        top_k = expert_ids.shape[1]
        local_exp = expert_w1.shape[0]
        cap_rows = capacity_rows(tok_dev, top_k, local_exp * ep_size)
        n_rows = local_exp * ep_size * cap_rows

        group_rows = lax.all_gather(tokens, "tp", axis=0, tiled=True)
        part_sum = swiglu_rows(group_rows, shared_w1, shared_w3, shared_w2)
        shared_out = lax.psum_scatter(part_sum, "tp", scatter_dimension=0, tiled=True)

        owner = expert_ids // local_exp
        row_code = (expert_ids % local_exp) * (ep_size * cap_rows) + owner * cap_rows + slots
        row_code = jnp.where(slots >= 0, row_code, n_rows)
        copy_tok = jnp.broadcast_to(jnp.arange(tok_dev, dtype=jnp.int32)[:, None], (tok_dev, top_k))
        inverse = jnp.full((n_rows,), tok_dev, jnp.int32).at[row_code.reshape(-1)].set(copy_tok.reshape(-1), mode="drop")
        send_rows = jnp.take(tokens, inverse, axis=0, mode="fill", fill_value=0).reshape(local_exp, ep_size, cap_rows, d_model)
        recv_rows = lax.all_to_all(send_rows, "ep", 1, 1, tiled=True)
        gate_pre = jnp.einsum("lscd,ldf->lscf", recv_rows, expert_w1, preferred_element_type=jnp.float32)
        up_pre = jnp.einsum("lscd,ldf->lscf", recv_rows, expert_w3, preferred_element_type=jnp.float32)
        hidden = (jax.nn.silu(gate_pre) * up_pre).astype(jnp.bfloat16)
        expert_out = jnp.einsum("lscf,lfd->lscd", hidden, expert_w2, preferred_element_type=jnp.float32).astype(jnp.bfloat16)
        back_rows = lax.all_to_all(expert_out, "ep", 1, 1, tiled=True).reshape(n_rows, d_model)
        routed = jnp.take(back_rows, row_code, axis=0, mode="fill", fill_value=0)
        routed_sum = jnp.sum(gates[:, :, None] * routed.astype(jnp.float32), axis=1)
        return (tokens.astype(jnp.float32) + shared_out + routed_sum).astype(jnp.bfloat16)

    return jax.shard_map(local_layer, mesh=mesh, in_specs=(row_spec, row_spec, row_spec, row_spec, P(None, "tp"), P(None, "tp"), P("tp", None), expert_spec, expert_spec, expert_spec), out_specs=row_spec, check_vma=False)
```

profile of v0, /device:TPU:1, one launch (start us, length us, event | category | flops | bytes accessed | tf_op | source)
XLA Modules:
  0.0 920.6 jit_solution(17648917678932900051)
XLA Ops:
  6.5 0.0 copy-start
  6.5 0.0 all-gather.2.cloned.1.call-start
  6.5 0.7 all-gather.2.cloned.1.call-update
  7.3 0.0 copy-start.4
  7.3 0.0 reduce-scatter.2.cloned.1.call-start
  7.3 159.3 %all-gather.2.cloned.1.call-done = bf16[6144,2048]{1,0:T(8,128)(2,1)} async-done(((bf16[384,2048]{1,0:T(8,128)(2,1)}), bf16[6144,2048]{1,0:T(8,128)(2,1)}) %all-gather.2.cloned.1.call-update) | async-done | bytes 25165840 | tf_op jit(solution)/shard_map/all_gather | solution.py:30
  166.7 18.8 %fusion.35 = f32[6144,176]{0,1:T(8,128)} fusion(bf16[6144,2048]{1,0:T(8,128)(2,1)} %all-gather.2.cloned.1.call-done, bf16[2048,176]{0,1:T(8,128)(2,1)} %param.14), kind=kOutput, calls=%fused_computation.51 | convolution fusion | flops 4429185024 | bytes 30212096 | tf_op jit(solution)/shard_map/dot_general | solution.py:12
  185.4 0.0 copy-done
  185.4 0.0 copy-done.4
  185.4 30.5 %fusion.14 = f32[6144,2048]{1,0:T(8,128)} fusion(bf16[176,2048]{1,0:T(8,128)(2,1)S(1)} %copy-done, bf16[6144,2048]{1,0:T(8,128)(2,1)} %all-gather.2.cloned.1.call-done, bf16[2048,176]{0,1:T(8,128)(2,1)S(1)} %copy-done.4, f32[6144,176]{0,1:T(8,128)} %fusion.35), kind=kOutput, calls=%fused_computation.17 | convolution fusion | flops 8864858112 | bytes 81264640 | tf_op jit(solution)/shard_map/dot_general | solution.py:15
  216.0 0.0 copy-start.9
  216.0 0.0 copy-start.10
  216.0 0.0 copy-start.2
  216.0 0.0 reduce-scatter.2.cloned.1.call-update
  216.0 0.7 copy-done.9
  216.7 0.0 copy-done.10
  216.7 0.6 compare_and_fusion.1
  217.3 0.0 copy-start.5
  217.3 0.1 copy.28
  217.4 0.2 reshape.55
  217.6 0.1 reshape.78
  217.8 19.5 %scatter_custom_fusion = s32[4608]{0:T(1024)S(1)} fusion(s32[2304]{0:T(1024)S(1)} %fusion.32, s32[2304]{0:T(1024)S(1)} %reshape.78, s32[]{:T(128)} %constant.69.clone.1), kind=kCustom, calls=%fused_computation.47 | custom fusion | bytes 18436 | tf_op jit(solution)/shard_map/scatter | solution.py:38
  237.4 0.0 copy-done.2
  237.4 18.3 %gather_fusion = bf16[4608,2048]{1,0:T(8,128)(2,1)} fusion(bf16[384,2048]{1,0:T(8,128)(2,1)S(1)} %copy-done.2, s32[5120]{0:T(1024)S(1)} %pad_clamp_fusion), kind=kCustom, calls=%fused_computation | custom fusion | bytes 37767168 | tf_op jit(solution)/shard_map/jit(_take)/gather | solution.py:39
  255.7 0.0 copy-done.5
  255.7 0.1 broadcast_in_dim.45
  255.9 9.5 %copy_select_fusion = bf16[8,8,72,2048]{3,2,0,1:T(8,128)(2,1)S(1)} fusion(bf16[8,8,72,2048]{3,2,1,0:T(8,128)(2,1)} %bitcast.28, pred[8,8,72]{2,0,1:T(8,128)(4,1)S(1)} %copy.29), kind=kLoop, calls=%fused_computation.11 | loop fusion | flops 9437184 | bytes 37753344 | tf_op jit(solution)/shard_map/jit(_take)/select_n | solution.py:39
  265.4 211.0 %all_to_all.10 = bf16[8,8,72,2048]{3,2,0,1:T(8,128)(2,1)} all-to-all(bf16[8,8,72,2048]{3,2,0,1:T(8,128)(2,1)S(1)} %copy_select_fusion), channel_id=1, replica_groups=mesh['dp'=1,'tp'=16,'ep'=8] {'ep'}, dimensions={1} | all-to-all | bytes 37748736 | tf_op jit(solution)/shard_map/all_to_all | solution.py:40
  476.4 39.0 %fusion.2 = f32[8,8,72,1408]{3,2,1,0:T(8,128)} fusion(bf16[8,2048,1408]{2,1,0:T(8,128)(2,1)} %param.18, bf16[8,8,72,2048]{3,2,0,1:T(8,128)(2,1)} %all_to_all.10), kind=kOutput, calls=%fused_computation.5 | convolution fusion | flops 26575110144 | bytes 90963968 | tf_op jit(solution)/shard_map/lscd,ldf->lscf/dot_general | solution.py:42
  515.3 48.2 %multiply_convert_fusion = bf16[8,8,72,1408]{3,2,1,0:T(8,128)(2,1)} fusion(f32[8,8,72,1408]{3,2,1,0:T(8,128)} %fusion.2, bf16[8,2048,1408]{2,1,0:T(8,128)(2,1)} %param.17, bf16[8,8,72,2048]{3,2,0,1:T(8,128)(2,1)} %all_to_all.10), kind=kOutput, calls=%fused_computation.9 | convolution fusion | flops 26614038528 | bytes 103940096 | tf_op jit(solution)/shard_map/lscd,ldf->lscf/dot_general | solution.py:41
  563.6 38.9 %fusion.10 = bf16[8,8,72,2048]{3,2,1,0:T(8,128)(2,1)} fusion(bf16[8,8,72,1408]{3,2,1,0:T(8,128)(2,1)} %multiply_convert_fusion, bf16[8,1408,2048]{2,1,0:T(8,128)(2,1)} %param.19), kind=kOutput, calls=%fused_computation.14 | convolution fusion | flops 26584547328 | bytes 77987840 | tf_op jit(solution)/shard_map/lscf,lfd->lscd/dot_general | solution.py:44
  602.5 16.9 %copy.33 = bf16[8,8,72,2048]{3,2,0,1:T(8,128)(2,1)} copy(bf16[8,8,72,2048]{3,2,1,0:T(8,128)(2,1)} %fusion.10) | data formatting | bytes 37748736 | tf_op jit(solution)/shard_map/convert_element_type | solution.py:44
  619.4 0.0 copy-start.6
  619.4 0.0 copy-start.8
  619.4 0.0 copy-start.7
  619.4 6.9 all-to-all-start.1
  626.4 0.0 copy-done.6
  626.4 0.1 copy.35
  626.5 0.1 reshape.68
  626.7 0.0 copy-done.8
  626.7 0.2 copy.27
  626.9 0.0 copy-done.7
  626.9 0.1 copy.26
  627.0 205.2 %all-to-all-done.1 = bf16[8,8,72,2048]{3,2,0,1:T(8,128)(2,1)} async-done(((bf16[8,8,72,2048]{3,2,0,1:T(8,128)(2,1)}), bf16[8,8,72,2048]{3,2,0,1:T(8,128)(2,1)}, u32[]{:S(2)}, u32[]{:S(2)}) %all-to-all-start.1) | async-done | bytes 18874400 | tf_op jit(solution)/shard_map/all_to_all | solution.py:45
  832.3 16.9 %copy.34 = bf16[8,8,72,2048]{3,2,1,0:T(8,128)(2,1)} copy(bf16[8,8,72,2048]{3,2,0,1:T(8,128)(2,1)} %all-to-all-done.1) | data formatting | bytes 37748736 | tf_op jit(solution)/shard_map/all_to_all | solution.py:45
  849.2 0.0 copy-start.1
  849.2 27.2 %gather_fusion.1 = bf16[2304,2048]{1,0:T(8,128)(2,1)} fusion(bf16[4608,2048]{1,0:T(8,128)(2,1)} %bitcast.27, s32[3072]{0:T(1024)S(1)} %pad_clamp_fusion.1), kind=kCustom, calls=%fused_computation.1 | custom fusion | bytes 18883584 | tf_op jit(solution)/shard_map/jit(_take)/gather | solution.py:46
  876.4 0.0 copy-start.3
  876.4 15.8 %reshape.67 = bf16[384,6,2048]{2,1,0:T(8,128)(2,1)} reshape(bf16[2304,2048]{1,0:T(8,128)(2,1)} %gather_fusion.1) | data formatting | bytes 18874368 | tf_op jit(solution)/shard_map/jit(_take)/gather | solution.py:46
  892.2 16.3 %multiply_reduce_fusion = f32[384,2048]{1,0:T(8,128)} fusion(bf16[384,6,2048]{2,1,0:T(8,128)(2,1)} %reshape.67, f32[384,6]{1,0:T(8,128)S(1)} %copy.26, pred[384,6]{1,0:T(8,128)(4,1)S(1)} %copy.27), kind=kLoop, calls=%fused_computation.10 | loop fusion | flops 18087936 | bytes 12594432 | tf_op jit(solution)/shard_map/reduce_sum | solution.py:47
  908.5 0.0 reduce-scatter.2.cloned.1.call-done
  908.5 0.0 copy-done.3
  908.5 4.8 add_convert_fusion
  913.3 0.0 copy-done.1
  (8 shorter events, 0.1 us)
Async XLA Ops:
  6.5 178.9 %copy-start = (bf16[176,2048]{1,0:T(8,128)(2,1)S(1)}, bf16[176,2048]{1,0:T(8,128)(2,1)}, u32[]{:S(2)}) copy-start(bf16[176,2048]{1,0:T(8,128)(2,1)} %param.16) | copy-start | bytes 2162692
  6.5 160.1 %all-gather.2.cloned.1.call-start = ((), (), s32[]{:S(2)}) async-start(), calls=%async_computation.3 | async-start | bytes 26738688 | tf_op jit(solution)/shard_map/all_gather | solution.py:30
  7.3 178.2 %copy-start.4 = (bf16[2048,176]{0,1:T(8,128)(2,1)S(1)}, bf16[2048,176]{0,1:T(8,128)(2,1)}, u32[]{:S(2)}) copy-start(bf16[2048,176]{0,1:T(8,128)(2,1)} %param.15) | copy-start | bytes 2162692
  7.3 901.2 %reduce-scatter.2.cloned.1.call-start = ((), (), s32[]{:S(2)}) async-start(), calls=%async_computation.4 | async-start | bytes 53477376 | tf_op jit(solution)/shard_map/reduce_scatter | solution.py:32
  216.0 0.7 copy-start.9
  216.0 0.7 copy-start.10
  216.0 21.4 %copy-start.2 = (bf16[384,2048]{1,0:T(8,128)(2,1)S(1)}, bf16[384,2048]{1,0:T(8,128)(2,1)}, u32[]{:S(2)}) copy-start(bf16[384,2048]{1,0:T(8,128)(2,1)} %param.10) | copy-start | bytes 4718596
  217.3 38.4 %copy-start.5 = (s32[384,6]{0,1:T(8,128)}, s32[384,6]{0,1:T(8,128)S(1)}, u32[]{:S(2)}) copy-start(s32[384,6]{0,1:T(8,128)S(1)} %get-tuple-element.6) | copy-start | bytes 27652
  619.4 6.9 copy-start.6
  619.4 7.2 copy-start.8
  619.4 7.4 copy-start.7
  619.4 212.8 %all-to-all-start.1 = ((bf16[8,8,72,2048]{3,2,0,1:T(8,128)(2,1)}), bf16[8,8,72,2048]{3,2,0,1:T(8,128)(2,1)}, u32[]{:S(2)}, u32[]{:S(2)}) async-start(bf16[8,8,72,2048]{3,2,0,1:T(8,128)(2,1)} %copy.33), calls=%async_computation.2 | async-start | bytes 37748736 | tf_op jit(solution)/shard_map/all_to_all | solution.py:45
  849.2 64.1 %copy-start.1 = (bf16[176,2048]{1,0:T(8,128)(2,1)S(1)}, bf16[176,2048]{1,0:T(8,128)(2,1)}, u32[]{:S(2)}) copy-start(bf16[176,2048]{1,0:T(8,128)(2,1)} %param.16) | copy-start | bytes 2162692
  876.4 32.1 %copy-start.3 = (bf16[384,2048]{1,0:T(8,128)(2,1)S(1)}, bf16[384,2048]{1,0:T(8,128)(2,1)}, u32[]{:S(2)}) copy-start(bf16[384,2048]{1,0:T(8,128)(2,1)} %param.10) | copy-start | bytes 4718596
Sparse Core Ops, SparseCore 0:
  9.5 157.1 all-gather.1
  216.1 279.2 reduce-scatter.1
where the time goes:
time: 925 us; the launch traced here: 921 us
  waiting for transfers between devices  365 us (39%)
  blocking collectives  211 us (23%)
  matrix products  175 us (19%)
  local copies, waits for them, and re-layouts  117 us (13%)
  other arithmetic  31.3 us (3%)
  between operations  13.9 us (2%)
    all_to_all x1, blocking collectives, local_layer(): recv_rows = lax.all_to_all(send_rows, 'ep', 1, 1, tiled=True)  211 us
    all_to_all x1, waiting for transfers between devices, local_layer(): lax.all_to_all(expert_out, 'ep', 1, 1, tiled=True).reshape(n_rows, d_model)  205 us
    all_gather x1, waiting for transfers between devices, local_layer(): group_rows = lax.all_gather(tokens, 'tp', axis=0, tiled=True)  159 us
    dot_general x1, matrix products, local_layer(): jnp.einsum('lscd,ldf->lscf', recv_rows, expert_w1, preferred_element_type...  48.2 us
    gather x2, local copies, waits for them, and re-layouts, local_layer(): routed = jnp.take(back_rows, row_code, axis=0, mode='fill', fill_value=0)  43 us
    dot_general x1, matrix products, local_layer(): jnp.einsum('lscd,ldf->lscf', recv_rows, expert_w3, preferred_element_type...  39 us
    dot_general x1, matrix products, local_layer(): jnp.einsum('lscf,lfd->lscd', hidden, expert_w2, preferred_element_type=jn...  38.9 us
    dot_general x1, matrix products, swiglu_rows(): return jnp.dot(hidden, w_down, preferred_element_type=jnp.float32)  30.5 us
  transfers between devices with their start and end apart: 3, of which 2 were waited for; matrix products, arithmetic and copies ran while one was open for 29% of the time, Pallas kernels for 0%

commit v1 on v0

v1 whole, which is shorter than its diff:
```python
import functools

import jax
import jax.numpy as jnp
from jax import lax
from jax.experimental import pallas as pl
from jax.experimental.pallas import tpu as pltpu
from jax.sharding import PartitionSpec as P

MESH = pl.DeviceIdType.MESH
ANY = pl.BlockSpec(memory_space=pl.ANY)
VM = pl.BlockSpec(memory_space=pltpu.VMEM)
F32 = jnp.float32
BF16 = jnp.bfloat16
DMA = pltpu.SemaphoreType.DMA
VMEM_CAP = 62 * 1024 * 1024
BF16_MAX = 3.3895313892515355e38


def capacity_rows(tok_dev, top_k, n_exp):
    return 8 * max(1, (2 * tok_dev * top_k + 8 * n_exp - 1) // (8 * n_exp))


def nt_dot(a, b):
    return lax.dot_general(a, b, (((1,), (1,)), ((), ())), preferred_element_type=F32)


def peer(k, q, n_ep):
    me = lax.axis_index("ep")
    chips = n_ep // 2
    chip, core = me // 2, lax.rem(me, 2)
    return lax.rem(chip + k, chips) * 2 + lax.rem(core + q, 2)


def meet(others):
    barrier = pltpu.get_barrier_semaphore()
    for other in others:
        pl.semaphore_signal(barrier, inc=1, device_id={"ep": other}, device_id_type=MESH)
    pl.semaphore_wait(barrier, len(others))


def send(src, dst, send_sem, recv_sem, to):
    copy = pltpu.make_async_remote_copy(src_ref=src, dst_ref=dst, send_sem=send_sem, recv_sem=recv_sem, device_id={"ep": to}, device_id_type=MESH)
    copy.start()
    return copy


def gather_kernel(dims, tok, cg, x_out, g_out, sib_out, tokbuf, cgbuf, oh, xst, gst, own_sem, cg_send, cg_recv, ring_send, fwd_send, sib_send, tok_recv, x_sem, g_sem, out_sem):
    n_ep, n_loc, cap, top_k = dims
    t_dev, d_model = tok.shape
    rows = n_loc * cap
    pr = t_dev // 4
    me = lax.axis_index("ep")
    sib = peer(0, 1, n_ep)
    right, left = peer(1, 0, n_ep), peer(3, 0, n_ep)
    own = pltpu.make_async_copy(tok, tokbuf.at[0], own_sem)
    own.start()
    cgbuf[0] = cg[...]
    pending = []
    meet([peer(r // 2, r % 2, n_ep) for r in range(1, n_ep)])

    def piece(r, p):
        return tokbuf.at[r, pl.ds(p * pr, pr), :]

    own.wait()
    for p, q in zip((0, 1, 2, 3), (2, 3, 0, 1)):
        pending.append(send(piece(0, p), piece(6, p), ring_send.at[0, p], tok_recv.at[6, p], right))
        pending.append(send(piece(0, q), piece(2, q), ring_send.at[1, q], tok_recv.at[2, q], left))
        pending.append(send(piece(0, p), piece(1, p), sib_send.at[0, p], tok_recv.at[1, p], sib))
        if p == 0:
            for r in range(1, n_ep):
                k, core = r // 2, r % 2
                back = 2 * ((n_ep // 2 - k) % (n_ep // 2)) + core
                pending.append(send(cg, cgbuf.at[back], cg_send.at[r], cg_recv.at[back], peer(k, core, n_ep)))

    def arrived(r, p):
        pltpu.make_async_copy(piece(r, p), piece(r, p), tok_recv.at[r, p]).wait()

    def relay(r, p):
        arrived(r, p)
        if r == 6 and p < 2:
            pending.append(send(piece(6, p), piece(4, p), fwd_send.at[p], tok_recv.at[4, p], right))
        if r == 2 and p >= 2:
            pending.append(send(piece(2, p), piece(4, p), fwd_send.at[p], tok_recv.at[4, p], left))
        pending.append(send(piece(r, p), piece(r + 1, p), sib_send.at[r // 2, p], tok_recv.at[r + 1, p], sib))

    def codes(r):
        if r:
            pltpu.make_async_copy(cgbuf.at[r], cgbuf.at[r], cg_recv.at[r]).wait()

    base = (me * rows).astype(F32)
    x_copies, g_copies = {}, {}

    def gather(r, slot):
        if slot in x_copies:
            x_copies[slot].wait()
        chunk = 2 * cap

        def one_hot(i, carry):
            place = lax.broadcasted_iota(jnp.int32, (chunk, t_dev), 0) + i * chunk
            want = place.astype(F32) + base
            hit = jnp.zeros((chunk, t_dev), F32)
            for j in range(top_k):
                hit = jnp.where(cgbuf[r, j : j + 1, :] == want, 1.0, hit)
            oh[pl.ds(pl.multiple_of(i * chunk, chunk), chunk), :] = hit.astype(BF16)
            return carry

        lax.fori_loop(0, rows // chunk, one_hot, 0)
        width = 512

        def product(n, carry):
            cols = pl.ds(pl.multiple_of(n * width, width), width)
            xst[slot, :, cols] = jnp.dot(oh[...], tokbuf[r, :, cols], preferred_element_type=F32).astype(BF16)
            return carry

        lax.fori_loop(0, d_model // width, product, 0)
        copy = pltpu.make_async_copy(xst.at[slot], x_out.at[r], x_sem.at[slot])
        copy.start()
        x_copies[slot] = copy

    def gates(r, slot):
        if slot in g_copies:
            g_copies[slot].wait()
        codes(r)
        both = cgbuf[r].T
        chunk = t_dev // 4

        def block(i, carry):
            place = lax.broadcasted_iota(jnp.int32, (chunk, rows), 1).astype(F32) + base
            at = pl.ds(pl.multiple_of(i * chunk, chunk), chunk)
            rows_cg = cgt[at, :]
            full = jnp.zeros((chunk, rows), F32)
            for j in range(top_k):
                full = jnp.where(rows_cg[:, j : j + 1] == place, rows_cg[:, 8 + j : 9 + j], full)
            first = jnp.minimum(full, BF16_MAX).astype(BF16)
            rest = full - first.astype(F32)
            second = rest.astype(BF16)
            third = (rest - second.astype(F32)).astype(BF16)
            gst[slot, at, 0:rows] = first
            gst[slot, at, rows : 2 * rows] = second
            gst[slot, at, 2 * rows : 3 * rows] = third
            return carry

        cgt = xgt
        cgt[...] = both
        lax.fori_loop(0, t_dev // chunk, block, 0)
        copy = pltpu.make_async_copy(gst.at[slot], g_out.at[r], g_sem.at[slot])
        copy.start()
        g_copies[slot] = copy

    xgt = out_sem[1]
    done_sem = out_sem[0]
    gates(0, 0)
    gather(0, 0)
    gates(1, 1)
    for p in range(4):
        arrived(1, p)
    sib_copy = pltpu.make_async_copy(tokbuf.at[1], sib_out, done_sem)
    sib_copy.start()
    gather(1, 1)
    relay(6, 0)
    relay(2, 2)
    gates(2, 0)
    gates(3, 1)
    relay(6, 1)
    relay(2, 3)
    gates(4, 0)
    gates(5, 1)
    gates(6, 0)
    gates(7, 1)
    relay(6, 2)
    relay(2, 0)
    relay(6, 3)
    relay(2, 1)
    gather(6, 0)
    gather(2, 1)
    for p in range(4):
        arrived(7, p)
    gather(7, 0)
    for p in range(4):
        arrived(3, p)
    gather(3, 1)
    for p in (0, 2, 1, 3):
        relay(4, p)
    gather(4, 0)
    for p in range(4):
        arrived(5, p)
    gather(5, 1)
    for copy in list(x_copies.values()) + list(g_copies.values()) + [sib_copy]:
        copy.wait()
    for copy in pending:
        copy.wait_send()


def gather_call(tokens, cg, n_ep, n_loc, cap, top_k):
    t_dev, d_model = tokens.shape
    rows = n_loc * cap

    def kernel(*refs):
        (tok, cgr, x_out, g_out, sib_out, tokbuf, cgbuf, oh, xst, gst, xgt, own_sem, cg_send, cg_recv, ring_send, fwd_send, sib_send, tok_recv, x_sem, g_sem, done_sem) = refs
        gather_kernel((n_ep, n_loc, cap, top_k), tok, cgr, x_out, g_out, sib_out, tokbuf, cgbuf, oh, xst, gst, own_sem, cg_send, cg_recv, ring_send, fwd_send, sib_send, tok_recv, x_sem, g_sem, (done_sem, xgt))

    return pl.pallas_call(
        kernel,
        name="gather_tokens",
        out_shape=(
            jax.ShapeDtypeStruct((n_ep, rows, d_model), BF16),
            jax.ShapeDtypeStruct((n_ep, t_dev, 3 * rows), BF16),
            jax.ShapeDtypeStruct((t_dev, d_model), BF16),
        ),
        in_specs=[ANY, VM],
        out_specs=(ANY, ANY, ANY),
        scratch_shapes=[
            pltpu.VMEM((n_ep, t_dev, d_model), BF16),
            pltpu.VMEM((n_ep, 16, t_dev), F32),
            pltpu.VMEM((rows, t_dev), BF16),
            pltpu.VMEM((2, rows, d_model), BF16),
            pltpu.VMEM((2, t_dev, 3 * rows), BF16),
            pltpu.VMEM((t_dev, 16), F32),
            DMA,
            DMA((n_ep,)),
            DMA((n_ep,)),
            DMA((2, 4)),
            DMA((4,)),
            DMA((4, 4)),
            DMA((n_ep, 4)),
            DMA((2,)),
            DMA((2,)),
            DMA,
        ],
        compiler_params=pltpu.CompilerParams(collective_id=0, has_side_effects=True, vmem_limit_bytes=VMEM_CAP),
    )(tokens, cg)


def hidden_call(x, w1, w3, cap):
    n_ep, rows, d_model = x.shape
    n_loc, _, ff = w1.shape
    m = n_ep * cap

    def kernel(x_ref, w1_ref, w3_ref, h_ref):
        xv = x_ref[...].reshape(m, d_model)
        for at in range(0, ff, 256):
            end = min(at + 256, ff)
            both = jnp.concatenate([w1_ref[:, at:end], w3_ref[:, at:end]], axis=1)
            pre = jnp.dot(xv, both, preferred_element_type=F32)
            h_ref[:, at:end] = (jax.nn.silu(pre[:, : end - at]) * pre[:, end - at :]).astype(BF16)

    return pl.pallas_call(
        kernel,
        name="expert_hidden",
        grid=(n_loc,),
        out_shape=jax.ShapeDtypeStruct((n_loc, m, ff), BF16),
        in_specs=[
            pl.BlockSpec((n_ep, cap, d_model), lambda e: (0, e, 0)),
            pl.BlockSpec((None, d_model, ff), lambda e: (e, 0, 0)),
            pl.BlockSpec((None, d_model, ff), lambda e: (e, 0, 0)),
        ],
        out_specs=pl.BlockSpec((None, m, ff), lambda e: (e, 0, 0)),
        compiler_params=pltpu.CompilerParams(vmem_limit_bytes=VMEM_CAP),
        cost_estimate=pl.CostEstimate(flops=4 * n_loc * m * d_model * ff, bytes_accessed=4 * n_loc * d_model * ff, transcendentals=0),
    )(x, w1, w3)


def combine_call(h, w2, g, hs, w2s, cap):
    n_loc, m, ff = h.shape
    n_ep, t_dev, k3 = g.shape
    d_model = w2.shape[2]
    rows = n_loc * cap
    ffs = hs.shape[1]
    width = 256

    def kernel(h_ref, w2_ref, g_ref, hs_ref, w2s_ref, p_ref, rbuf):
        def down(e, carry):
            r = jnp.dot(h_ref[e], w2_ref[e], preferred_element_type=F32).astype(BF16).astype(F32)
            rbuf[:, pl.ds(pl.multiple_of(e * cap, cap), cap), :] = r.reshape(n_ep, cap, width)
            return carry

        lax.fori_loop(0, n_loc, down, 0)

        def add_up(r, carry):
            rr = rbuf[r].astype(BF16)
            p_ref[r] = jnp.dot(g_ref[r], jnp.concatenate([rr, rr, rr], axis=0), preferred_element_type=F32)
            return carry

        lax.fori_loop(0, n_ep, add_up, 0)
        for q in range(2):
            p_ref[q] += jnp.dot(hs_ref[q * t_dev : (q + 1) * t_dev, :], w2s_ref[...], preferred_element_type=F32)

    once = pl.Buffered(1)
    return pl.pallas_call(
        kernel,
        name="combine",
        grid=(d_model // width,),
        out_shape=jax.ShapeDtypeStruct((d_model // width, n_ep, t_dev, width), F32),
        in_specs=[
            pl.BlockSpec((n_loc, m, ff), lambda b: (0, 0, 0), pipeline_mode=once),
            pl.BlockSpec((n_loc, ff, width), lambda b: (0, 0, b)),
            pl.BlockSpec((n_ep, t_dev, k3), lambda b: (0, 0, 0), pipeline_mode=once),
            pl.BlockSpec((2 * t_dev, ffs), lambda b: (0, 0), pipeline_mode=once),
            pl.BlockSpec((ffs, width), lambda b: (0, b)),
        ],
        out_specs=pl.BlockSpec((None, n_ep, t_dev, width), lambda b: (b, 0, 0, 0)),
        scratch_shapes=[pltpu.VMEM((n_ep, rows, width), F32)],
        compiler_params=pltpu.CompilerParams(vmem_limit_bytes=VMEM_CAP),
        cost_estimate=pl.CostEstimate(flops=2 * n_loc * m * d_model * ff, bytes_accessed=2 * n_loc * d_model * ff, transcendentals=0),
    )(h, w2, g, hs, w2s)


def return_call(parts, tokens, n_ep):
    n_blk, _, t_dev, width = parts.shape
    d_model = tokens.shape[1]
    half = n_blk // 2
    order = [b for pair in zip(range(half), range(half, n_blk)) for b in pair]

    def kernel(p, tok, out, ploc, sibrecv, d2recv, finrecv, ld_sem, sib_send, sib_recv, d2_send, d2_recv, fin_send, fin_recv):
        sib = peer(0, 1, n_ep)
        right, left = peer(1, 0, n_ep), peer(3, 0, n_ep)
        loads = {}
        for b in order:
            for k in (2, 1, 3, 0):
                loads[k, b] = pltpu.make_async_copy(p.at[b, 2 * k], ploc.at[k, b], ld_sem.at[k, b])
        meet([sib, right, left])
        pending = []
        for b in order:
            for k in (2, 1, 3, 0):
                loads[k, b].start()
                pending.append(send(p.at[b, 2 * k + 1], sibrecv.at[k, b], sib_send.at[k, b], sib_recv.at[k, b], sib))

        def merge(k, b):
            loads[k, b].wait()
            pltpu.make_async_copy(sibrecv.at[k, b], sibrecv.at[k, b], sib_recv.at[k, b]).wait()
            ploc[k, b] += sibrecv[k, b]

        def pass_on(b):
            k, to, side = (1, right, 0) if b < half else (3, left, 1)
            pltpu.make_async_copy(d2recv.at[b], d2recv.at[b], d2_recv.at[b]).wait()
            ploc[k, b] += d2recv[b]
            pending.append(send(ploc.at[k, b], finrecv.at[side, b], fin_send.at[side, b], fin_recv.at[side, b], to))

        for i, b in enumerate(order):
            to = right if b < half else left
            merge(2, b)
            pending.append(send(ploc.at[2, b], d2recv.at[b], d2_send.at[b], d2_recv.at[b], to))
            merge(1, b)
            merge(3, b)
            if b < half:
                pending.append(send(ploc.at[3, b], finrecv.at[1, b], fin_send.at[1, b], fin_recv.at[1, b], left))
            else:
                pending.append(send(ploc.at[1, b], finrecv.at[0, b], fin_send.at[0, b], fin_recv.at[0, b], right))
            merge(0, b)
            if i >= 2:
                pass_on(order[i - 2])
        pass_on(order[-2])
        pass_on(order[-1])
        for b in order:
            cols = pl.ds(b * width, width)
            for side in range(2):
                pltpu.make_async_copy(finrecv.at[side, b], finrecv.at[side, b], fin_recv.at[side, b]).wait()
            out[:, cols] = (tok[:, cols].astype(F32) + ploc[0, b] + (finrecv[0, b] + finrecv[1, b])).astype(BF16)
        for copy in pending:
            copy.wait_send()

    return pl.pallas_call(
        kernel,
        name="return_sums",
        out_shape=jax.ShapeDtypeStruct((t_dev, d_model), BF16),
        in_specs=[ANY, VM],
        out_specs=VM,
        scratch_shapes=[
            pltpu.VMEM((4, n_blk, t_dev, width), F32),
            pltpu.VMEM((4, n_blk, t_dev, width), F32),
            pltpu.VMEM((n_blk, t_dev, width), F32),
            pltpu.VMEM((2, n_blk, t_dev, width), F32),
            DMA((4, n_blk)),
            DMA((4, n_blk)),
            DMA((4, n_blk)),
            DMA((n_blk,)),
            DMA((n_blk,)),
            DMA((2, n_blk)),
            DMA((2, n_blk)),
        ],
        compiler_params=pltpu.CompilerParams(collective_id=1, has_side_effects=True, vmem_limit_bytes=VMEM_CAP),
    )(parts, tokens)


def solution(mesh):
    n_ep = mesh.shape["ep"]
    row_spec = P(("dp", "ep", "tp"), None)
    expert_spec = P("ep", None, None)

    def local_layer(tokens, expert_ids, gates, slots, shared_w1, shared_w3, shared_w2, expert_w1, expert_w3, expert_w2):
        t_dev, d_model = tokens.shape
        top_k = expert_ids.shape[1]
        n_loc = expert_w1.shape[0]
        cap = capacity_rows(t_dev, top_k, n_loc * n_ep)
        ffs = shared_w1.shape[1] // 2
        core = lax.rem(lax.axis_index("ep"), 2)

        mine = [lax.dynamic_slice_in_dim(w, core * ffs, ffs, 0) for w in (shared_w1.T, shared_w3.T, shared_w2)]
        ws = lax.all_gather(jnp.concatenate(mine, axis=0), "tp", axis=0, tiled=False)
        w1s, w3s, w2s = (ws[:, i * ffs : (i + 1) * ffs, :].reshape(-1, d_model) for i in range(3))

        code = jnp.where(slots >= 0, expert_ids * cap + slots, -1).astype(F32)
        pad = jnp.zeros((8 - top_k, t_dev), F32)
        cg = jnp.concatenate([code.T, pad - 1.0, gates.T, pad], axis=0)
        x, g, tok_sib = gather_call(tokens, cg, n_ep, n_loc, cap, top_k)
        h = hidden_call(x, expert_w1, expert_w3, cap)
        both = jnp.concatenate([tokens, tok_sib], axis=0)
        hs = (jax.nn.silu(nt_dot(both, w1s)) * nt_dot(both, w3s)).astype(BF16)
        parts = combine_call(h, expert_w2, g, hs, w2s, cap)
        return return_call(parts, tokens, n_ep)

    return jax.shard_map(local_layer, mesh=mesh, in_specs=(row_spec, row_spec, row_spec, row_spec, P(None, "tp"), P(None, "tp"), P("tp", None), expert_spec, expert_spec, expert_spec), out_specs=row_spec, check_vma=False)
```

time: 925 us -> 381 us (0.41)
  waiting for transfers between devices: 365 us -> 0.02 us
  Pallas kernels: 0 us -> 331 us
  blocking collectives: 211 us -> 0 us
  matrix products: 175 us -> 15.5 us
  local copies, waits for them, and re-layouts: 117 us -> 18.6 us
  other arithmetic: 31.3 us -> 1.73 us
    pallas_call x0 -> x4, Pallas kernels: none -> 331 us  [the longest x1 111 us: return_call(): pl.pallas_call(kernel, name='return_sums', out_shape=jax.ShapeDtypeStruct...]
    all_to_all x1 -> x0, blocking collectives: 211 us -> none  [local_layer(): recv_rows = lax.all_to_all(send_rows, 'ep', 1, 1, tiled=True)]
    all_to_all x1 -> x0, waiting for transfers between devices: 205 us -> none  [local_layer(): lax.all_to_all(expert_out, 'ep', 1, 1, tiled=True).reshape(n_rows, d_model)]
    dot_general x5 -> x2, matrix products: 175 us -> 15.5 us  [nt_dot(): lax.dot_general(a, b, (((1,), (1,)), ((), ())), preferred_element_type=F32)]
    all_gather x1, waiting for transfers between devices: 159 us -> 0.01 us  [local_layer(): lax.all_gather(jnp.concatenate(mine, axis=0), 'tp', axis=0, tiled=False)]
    gather x3 -> x0, local copies, waits for them, and re-layouts: 61.3 us -> none  [the longest x2 43 us: local_layer(): routed = jnp.take(back_rows, row_code, axis=0, mode='fill', fill_value=0)]
    scatter x1 -> x0, local copies, waits for them, and re-layouts: 19.5 us -> none  [local_layer(): jnp.full((n_rows,), tok_dev, jnp.int32).at[row_code.reshape(-1)]]
    all_to_all x1 -> x0, local copies, waits for them, and re-layouts: 16.9 us -> none  [local_layer(): lax.all_to_all(expert_out, 'ep', 1, 1, tiled=True).reshape(n_rows, d_model)]
  transfers between devices with their start and end apart: 3 -> 1, of which waited for: 2 -> 0; matrix products, arithmetic and copies ran while one was open for 29% -> 1% of each run, Pallas kernels for 0% -> 34%
where the time goes in v1:
time: 381 us
  Pallas kernels  331 us (87%)
  local copies, waits for them, and re-layouts  18.6 us (5%)
  matrix products  15.5 us (4%)
  between operations  13.5 us (4%)
    pallas_call x1, Pallas kernels, return_call(): pl.pallas_call(kernel, name='return_sums', out_shape=jax.ShapeDtypeStruct...  111 us
    pallas_call x1, Pallas kernels, combine_call(): pl.pallas_call(kernel, name='combine', grid=(d_model // width,), out_shap...  92.4 us
    pallas_call x1, Pallas kernels, gather_call(): pl.pallas_call(kernel, name='gather_tokens', out_shape=(jax.ShapeDtypeStr...  66.4 us
    pallas_call x1, Pallas kernels, hidden_call(): pl.pallas_call(kernel, name='expert_hidden', grid=(n_loc,), out_shape=jax...  61.3 us
    dot_general x2, matrix products, nt_dot(): lax.dot_general(a, b, (((1,), (1,)), ((), ())), preferred_element_type=F32)  15.5 us
    slice x1, local copies, waits for them, and re-layouts, local_layer(): ws[:, i * ffs:(i + 1) * ffs, :].reshape(-1, d_model)  9.23 us
  transfers between devices with their start and end apart: 1, of which 0 were waited for; matrix products, arithmetic and copies ran while one was open for 1% of the time, Pallas kernels for 34%

profile of v1, /device:TPU:1, one launch (start us, length us, event | category | flops | bytes accessed | tf_op | source)
XLA Modules:
  0.0 380.6 jit_solution(7870858877787087894)
XLA Ops:
  6.5 0.0 copy-start
  6.5 0.0 copy-start.3
  6.5 0.0 copy-start.4
  6.5 0.0 copy-start.5
  6.5 0.0 all-gather.3.cloned.1.call-start
  6.6 1.1 copy-done
  7.7 0.0 copy-start.2
  7.7 1.3 dynamic-slice_bitcast_fusion
  9.0 1.1 pad_maximum_fusion
  10.0 0.0 all-gather.3.cloned.1.call-update
  10.0 0.1 pad.4.clone
  10.1 0.1 pad.6.clone
  10.2 0.0 copy-done.3
  10.2 0.0 copy-done.4
  10.2 0.0 copy-done.5
  10.2 0.7 maximum_maximum_fusion.refs_1_
  10.9 66.4 %gather_tokens.1 = (bf16[8,576,2048]{2,1,0:T(8,128)(2,1)}, bf16[8,384,1728]{2,1,0:T(8,128)(2,1)}, bf16[384,2048]{1,0:T(8,128)(2,1)}) custom-call(bf16[384,2048]{1,0:T(8,128)(2,1)} %tok.1, f32[16,384]{1,0:T(8,128)} %maximum_maximum_fusion.refs_1_), custom_call_target="tpu_custom_call" | custom-call | tf_op jit(solution)/shard_map/gather_tokens/pallas_call | solution.py:203
  77.3 0.0 copy-done.2
  77.3 1.3 constant_dynamic-update-slice_fusion.1
  78.6 2.7 constant_dynamic-update-slice_fusion
  81.4 61.3 %expert_hidden.1.h_ref = bf16[8,576,1408]{2,1,0:T(8,128)(2,1)} custom-call(bf16[8,576,2048]{2,1,0:T(8,128)(2,1)} %get-tuple-element.8.x_ref, bf16[8,2048,1408]{2,1,0:T(8,128)(2,1)} %w1_ref.1, bf16[8,2048,1408]{2,1,0:T(8,128)(2,1)} %w3_ref.1), custom_call_target="tpu_custom_call" | custom-call | flops 53150220288 | bytes 92274688 | tf_op jit(solution)/shard_map/expert_hidden/pallas_call | solution.py:248
  142.6 0.0 all-gather.3.cloned.1.call-done
  142.6 9.2 %fusion = (bf16[16,88,2048]{2,1,0:T(8,128)(2,1)}, bf16[16,88,2048]{2,1,0:T(8,128)(2,1)S(1)}, bf16[16,88,2048]{2,1,0:T(8,128)(2,1)S(1)}) fusion(bf16[16,264,2048]{2,1,0:T(8,128)(2,1)} %bitcast.16), kind=kLoop, calls=%fused_computation.9 | loop fusion | bytes 34603008 | tf_op jit(solution)/shard_map/slice | solution.py:401
  151.9 6.9 %fusion.1 = f32[768,1408]{1,0:T(8,128)S(1)} fusion(bf16[768,2048]{1,0:T(8,128)(2,1)} %constant_dynamic-update-slice_fusion, bf16[1408,2048]{1,0:T(8,128)(2,1)S(1)} %bitcast.18), kind=kOutput, calls=%fused_computation.10 | convolution fusion | flops 4429185024 | bytes 13238272 | tf_op jit(solution)/shard_map/dot_general | solution.py:25
  158.8 8.6 %multiply_convert_fusion.hs_ref = bf16[768,1408]{1,0:T(8,128)(2,1)} fusion(f32[768,1408]{1,0:T(8,128)S(1)} %fusion.1, bf16[768,2048]{1,0:T(8,128)(2,1)} %constant_dynamic-update-slice_fusion, bf16[1408,2048]{1,0:T(8,128)(2,1)S(1)} %bitcast.17), kind=kOutput, calls=%fused_computation | convolution fusion | flops 4435673088 | bytes 15400960 | tf_op jit(solution)/shard_map/dot_general | solution.py:25
  167.4 92.4 %combine.1.p = f32[8,8,384,256]{3,2,1,0:T(8,128)} custom-call(bf16[8,576,1408]{2,1,0:T(8,128)(2,1)} %expert_hidden.1.h_ref, bf16[8,1408,2048]{2,1,0:T(8,128)(2,1)} %w2_ref.1, bf16[8,384,1728]{2,1,0:T(8,128)(2,1)} %get-tuple-element.9.g_ref, bf16[768,1408]{1,0:T(8,128)(2,1)} %multiply_convert_fusion.hs_ref, bf16[1408,2048]{1,0:T(8,128)(2,1)} %bitcast.15), custom_call_target="tpu_custom_call" | custom-call | flops 26575110144 | bytes 46137344 | tf_op jit(solution)/shard_map/combine/pallas_call | solution.py:290
  259.8 0.0 copy-start.1
  259.8 111.2 %return_sums.1 = bf16[384,2048]{1,0:T(8,128)(2,1)} custom-call(f32[8,8,384,256]{3,2,1,0:T(8,128)} %combine.1.p, bf16[384,2048]{1,0:T(8,128)(2,1)} %tok.1), custom_call_target="tpu_custom_call" | custom-call | tf_op jit(solution)/shard_map/return_sums/pallas_call | solution.py:363
  371.0 2.7 copy.13
  373.8 0.0 copy-done.1
  (4 shorter events, 0.0 us)
Async XLA Ops:
  6.5 1.1 copy-start
  6.5 3.7 copy-start.3
  6.5 3.7 copy-start.4
  6.5 3.7 copy-start.5
  6.5 136.1 %all-gather.3.cloned.1.call-start = ((), (), s32[]{:S(2)}) async-start(), calls=%async_computation | async-start | bytes 18382848 | tf_op jit(solution)/shard_map/all_gather | solution.py:400
  7.7 69.6 %copy-start.2 = (bf16[384,2048]{1,0:T(8,128)(2,1)S(1)}, bf16[384,2048]{1,0:T(8,128)(2,1)}, u32[]{:S(2)}) copy-start(bf16[384,2048]{1,0:T(8,128)(2,1)} %tok.1) | copy-start | bytes 4718596
  259.8 114.0 %copy-start.1 = (bf16[176,2048]{1,0:T(8,128)(2,1)S(1)}, bf16[176,2048]{1,0:T(8,128)(2,1)}, u32[]{:S(2)}) copy-start(bf16[176,2048]{1,0:T(8,128)(2,1)} %param.16) | copy-start | bytes 2162692
Sparse Core Ops, SparseCore 0:
  10.2 116.9 all-gather.2
